TPU v7x, 32 devices: a whole 2x2x4 slice. The times are simulated.
32 devices in a mesh: band: 8 (over z, x), grid: 4 (over y, core).
Axes of the slice: x: 2, y: 2, z: 4, core: 2. Of those that a mesh axis runs over, the one named last changes fastest.
Arguments:
- partial_density: float32 [8, 128, 128, 128], P('band', 'grid'), may hold values from 0.01 to 1
- node_index: int32 [128, 128, 128], P('grid'), may hold values from 0 to 19
- node_weight: float32 [4, 128, 128, 128], P(None, 'grid'), may hold values from 0 to 1
- node_slope: float32 [4, 128, 128, 128], P(None, 'grid'), may hold values from -6 to 6
- kernel_table: float32 [20, 20, 114], replicated, may hold values from -0.8 to 0.8, as said below
Outputs:
- potential: float32 [128, 128, 128], P('grid')
Inputs may be any that keep to these rules, and one draw needn't show every extreme that they name: node_index(r) is the node at the lower end of the interval of q0 at r; nodes node_index - 1 to node_index + 2 carry the four weights. `kernel_table`: symmetric in its first two indices.
All inputs are finite; a program needn't handle non-finite values.
Results may differ from a plain program's by a relative error of at most 0.0003.
Values sent between devices are 32-bit elements; how exact they have to be, the bound alone decides.
A program may use at most 128 MiB of HBM per device.

v0:
```python
import math
import jax
import jax.numpy as jnp
from jax import lax
from jax.sharding import PartitionSpec as P

N = 128


def frequency_of(positions, length):
    return jnp.where(positions < length // 2, positions, positions - length)


def shell_split(square_norm):
    root_value = jnp.sqrt(square_norm.astype(jnp.float32))
    shell_idx = root_value.astype(jnp.int32)
    shell_idx = shell_idx - (shell_idx * shell_idx > square_norm).astype(jnp.int32)
    shell_idx = shell_idx + ((shell_idx + 1) * (shell_idx + 1) <= square_norm).astype(jnp.int32)
    fraction = root_value - shell_idx.astype(jnp.float32)
    return (shell_idx, fraction)


def node_fields(count_nodes, intervals, weights):
    node_ids = jnp.arange(count_nodes, dtype=jnp.int32)
    summed = jnp.zeros((count_nodes,) + intervals.shape, jnp.float32)
    for offset in range(4):
        matched = node_ids[:, None, None, None] == (intervals + (offset - 1))[None]
        summed = summed + jnp.where(matched, weights[offset][None], jnp.zeros((), jnp.float32))
    return summed


def phase_table(source_idx, target_idx, modulus):
    product_mod = source_idx[:, None] * target_idx[None, :] % modulus
    angles = product_mod.astype(jnp.float32) * (2.0 * math.pi / modulus)
    return (jnp.cos(angles), jnp.sin(angles))


def contract(pattern, operand, matrix):
    return jnp.einsum(pattern, operand, matrix, precision=lax.Precision.HIGHEST)


def mirrored(values, dim):
    return jnp.roll(jnp.flip(values, dim), 1, dim)


def forward_tables(positions, plane_ids, length):
    cosine, sine = phase_table(positions, plane_ids, length)
    alternating = jnp.where(positions % 2 == 0, 1.0, -1.0).astype(jnp.float32)
    sine = jnp.where(plane_ids[None, :] == 0, -alternating[:, None], sine)
    return (cosine, sine)


def shell_weights_of(square_norm, shell_count):
    shell_ids = jnp.arange(shell_count, dtype=jnp.int32)
    shell_idx, fraction = shell_split(square_norm)
    expand = (slice(None),) + (None,) * square_norm.ndim
    lower_hit = shell_ids[expand] == shell_idx[None]
    upper_hit = shell_ids[expand] == shell_idx[None] + 1
    return jnp.where(lower_hit, 1.0 - fraction[None], 0.0) + jnp.where(
        upper_hit, fraction[None], 0.0
    )


def per_device(partial_density, node_index, node_weight, node_slope, kernel_table):
    length = N
    half = length // 2
    count_nodes = kernel_table.shape[0]
    shell_count = kernel_table.shape[2]
    planes = half // lax.axis_size("band")
    grid_part = length // lax.axis_size("grid")
    band_at = lax.axis_index("band")
    grid_at = lax.axis_index("grid")
    full_range = jnp.arange(length, dtype=jnp.int32)
    own_planes = band_at * planes + jnp.arange(planes, dtype=jnp.int32)
    own_rows = grid_at * grid_part + jnp.arange(grid_part, dtype=jnp.int32)
    first_band = band_at == 0
    lower_rows = (full_range >= 1) & (full_range < half)
    upper_rows = full_range > half
    density = lax.psum(partial_density[0], "band")
    theta_fields = density[None] * node_fields(count_nodes, node_index, node_weight)
    cosine_z, sine_z = forward_tables(full_range, own_planes, length)
    forward_real = contract("axyz,zk->axyk", theta_fields, cosine_z)
    forward_imag = -contract("axyz,zk->axyk", theta_fields, sine_z)
    columns = jnp.stack([forward_real, forward_imag])
    cosine_full, sine_full = phase_table(full_range, full_range, length)
    y_cos = contract("caxyp,yw->caxpw", columns, cosine_full)
    y_sin = contract("caxyp,yw->caxpw", columns, sine_full)
    ywave_real = y_cos[0] + y_sin[1]
    ywave_imag = y_cos[1] - y_sin[0]
    first_real = ywave_real[:, :, 0, :]
    first_imag = ywave_imag[:, :, 0, :]
    turned_real = mirrored(first_real, 2)
    turned_imag = mirrored(first_imag, 2)
    packed_real = jnp.where(
        lower_rows,
        0.5 * (first_real + turned_real),
        jnp.where(upper_rows, 0.5 * (turned_imag + first_imag), first_real),
    )
    packed_imag = jnp.where(
        lower_rows,
        0.5 * (first_imag - turned_imag),
        jnp.where(upper_rows, 0.5 * (first_real - turned_real), first_imag),
    )
    ywave_real = ywave_real.at[:, :, 0, :].set(jnp.where(first_band, packed_real, first_real))
    ywave_imag = ywave_imag.at[:, :, 0, :].set(jnp.where(first_band, packed_imag, first_imag))
    pencils = lax.all_to_all(
        jnp.stack([ywave_real, ywave_imag]), "grid", split_axis=4, concat_axis=2, tiled=True
    )
    x_cos = contract("caxpw,xv->capwv", pencils, cosine_full)
    x_sin = contract("caxpw,xv->capwv", pencils, sine_full)
    spec_real = x_cos[0] + x_sin[1]
    spec_imag = x_cos[1] - x_sin[0]
    freq_x = frequency_of(full_range, length)
    square_x = freq_x * freq_x
    freq_rows = frequency_of(own_rows, length)
    plane_square = own_planes * own_planes
    third_square = jnp.where(
        (own_planes[:, None] == 0) & (own_rows[None, :] > half), half * half, plane_square[:, None]
    )
    special_rows = ((own_rows == 0) | (own_rows == half)) & (own_planes[0] == 0)

    def mix_row(row_idx):
        row_real = lax.dynamic_index_in_dim(spec_real, row_idx, 2, keepdims=False)
        row_imag = lax.dynamic_index_in_dim(spec_imag, row_idx, 2, keepdims=False)
        freq_row = lax.dynamic_index_in_dim(freq_rows, row_idx, 0, keepdims=False)
        third_row = lax.dynamic_index_in_dim(third_square, row_idx, 1, keepdims=False)
        square_norm = third_row[:, None] + square_x[None, :] + freq_row * freq_row
        kernel = contract("abs,spx->abpx", kernel_table, shell_weights_of(square_norm, shell_count))
        out_real = contract("abpx,apx->bpx", kernel, row_real)
        out_imag = contract("abpx,apx->bpx", kernel, row_imag)
        other_norm = square_x + freq_row * freq_row + half * half
        kernel_other = contract(
            "abs,sx->abx", kernel_table, shell_weights_of(other_norm, shell_count)
        )
        flag = lax.dynamic_index_in_dim(special_rows, row_idx, 0, keepdims=False).astype(
            jnp.float32
        )
        spread = 0.5 * flag * (kernel[:, :, 0, :] - kernel_other)
        base_real = row_real[:, 0, :]
        base_imag = row_imag[:, 0, :]
        delta_real = mirrored(base_real, 1) - base_real
        delta_imag = -mirrored(base_imag, 1) - base_imag
        out_real = out_real.at[:, 0, :].add(contract("abx,ax->bx", spread, delta_real))
        out_imag = out_imag.at[:, 0, :].add(contract("abx,ax->bx", spread, delta_imag))
        return jnp.stack([out_real, out_imag])

    mixed = lax.map(mix_row, jnp.arange(grid_part, dtype=jnp.int32))
    i_cos = contract("wcbpx,xv->wcbpv", mixed, cosine_full)
    i_sin = contract("wcbpx,xv->wcbpv", mixed, sine_full)
    inverse_real = i_cos[:, 0] - i_sin[:, 1]
    inverse_imag = i_cos[:, 1] + i_sin[:, 0]
    returned = lax.all_to_all(
        jnp.stack([inverse_real, inverse_imag], axis=1),
        "grid",
        split_axis=4,
        concat_axis=0,
        tiled=True,
    )
    lower_col = lower_rows[:, None, None]
    upper_col = upper_rows[:, None, None]
    back_real = returned[:, 0, :, 0, :]
    back_imag = returned[:, 1, :, 0, :]
    flip_real = mirrored(back_real, 0)
    flip_imag = mirrored(back_imag, 0)
    joined_real = jnp.where(
        lower_col, back_real - flip_imag, jnp.where(upper_col, flip_real + back_imag, back_real)
    )
    joined_imag = jnp.where(
        lower_col, back_imag + flip_real, jnp.where(upper_col, back_real - flip_imag, back_imag)
    )
    returned = returned.at[:, 0, :, 0, :].set(jnp.where(first_band, joined_real, back_real))
    returned = returned.at[:, 1, :, 0, :].set(jnp.where(first_band, joined_imag, back_imag))
    b_cos = contract("wcbpx,wy->cbpxy", returned, cosine_full)
    b_sin = contract("wcbpx,wy->cbpxy", returned, sine_full)
    slab_real = b_cos[0] - b_sin[1]
    slab_imag = b_cos[1] + b_sin[0]
    cosine_own, sine_own = phase_table(own_planes, full_range, length)
    alternating = jnp.where(full_range % 2 == 0, 1.0, -1.0).astype(jnp.float32)
    cosine_back = jnp.where(own_planes[:, None] == 0, 1.0, 2.0 * cosine_own)
    sine_back = jnp.where(own_planes[:, None] == 0, -alternating[None, :], 2.0 * sine_own)
    scale_factor = 1.0 / float(length) ** 3
    field_parts = (
        contract("bpxy,pz->bxyz", slab_real, cosine_back)
        - contract("bpxy,pz->bxyz", slab_imag, sine_back)
    ) * scale_factor
    slopes = node_fields(count_nodes, node_index, node_slope)
    partial_potential = jnp.sum(field_parts * slopes, axis=0)
    return lax.psum(partial_potential, "band")


def solution(mesh):
    placed = (
        P("band", "grid", None, None),
        P("grid", None, None),
        P(None, "grid", None, None),
        P(None, "grid", None, None),
        P(),
    )
    return jax.shard_map(
        per_device, mesh=mesh, in_specs=placed, out_specs=P("grid", None, None), check_vma=False
    )
```

profile of v0, /device:TPU:0, one launch (start us, length us, event | category | flops | bytes accessed | tf_op | source)
XLA Modules:
  0.0 1415.7 jit_solution(10311914120012794032)
XLA Ops:
  17.1 98.9 %all-reduce.3.cloned.1.call-done = f32[32,128,128]{2,1,0:T(8,128)} async-done(((f32[32,128,128]{2,1,0:T(8,128)}), f32[32,128,128]{2,1,0:T(8,128)}) %all-reduce.3.cloned.1.call-update) | async-done | bytes 2097168 | tf_op jit(solution)/shard_map/psum | solution.py:79
  116.0 66.0 %fusion.70 = f32[1,20,32,128,8]{3,4,2,1,0:T(8,128)} fusion(f32[32,128,128]{2,1,0:T(8,128)} %get-tuple-element.295, s32[32,128,128]{2,1,0:T(8,128)} %get-tuple-element.309, f32[32,128,128]{2,1,0:T(8,128)} %get-tuple-element.296, s32[32,128,128]{2,1,0:T(8,128)} %get-tuple-element.310, f32[32,128,128]{2,1,0:T(8,128)} %get-tuple-element.294, ...), kind=kOutput, calls=%fused_computation.132 | convolution fusion | flops 1132476416 | bytes 21495840 | tf_op jit(solution)/shard_map/axyz,zk->axyk/dot_general | solution.py:39
  182.0 57.5 %negate_bitcast_fusion = f32[1,20,32,128,8]{3,4,2,1,0:T(8,128)} fusion(f32[32,128,128]{2,1,0:T(8,128)} %get-tuple-element.295, s32[32,128,128]{2,1,0:T(8,128)} %get-tuple-element.309, f32[32,128,128]{2,1,0:T(8,128)} %get-tuple-element.296, s32[32,128,128]{2,1,0:T(8,128)} %get-tuple-element.310, f32[32,128,128]{2,1,0:T(8,128)} %get-tuple-element.294, ...), kind=kOutput, calls=%fused_computation.123 | convolution fusion | flops 1133132800 | bytes 21496360 | tf_op jit(solution)/shard_map/axyz,zk->axyk/dot_general | solution.py:39
  266.0 7.4 scatter.15
  273.4 9.3 scatter.14
  287.3 17.6 %copy.61 = f32[2,20,32,8,128]{2,3,1,0,4:T(8,128)} copy(f32[2,20,32,8,128]{4,3,2,1,0:T(8,128)} %pad_maximum_fusion.1) | data formatting | bytes 10485760 | tf_op jit(solution)/shard_map/stack | solution.py:107
  304.9 23.5 %reshape.667 = f32[4,1,327680]{2,1,0:T(1,128)} reshape(f32[128,2,20,8,32]{4,3,2,1,0:T(8,128)} %bitcast.306) | data formatting | bytes 10485760
  333.6 59.3 %all-to-all-done = f32[4,1,327680]{2,1,0:T(1,128)} async-done(((f32[4,1,327680]{2,1,0:T(1,128)}), f32[4,1,327680]{2,1,0:T(1,128)}, u32[]{:S(2)}, u32[]{:S(2)}) %all-to-all-start) | async-done | bytes 5242912 | tf_op jit(solution)/shard_map/all_to_all | solution.py:106
  393.5 17.9 %reduce.21 = f32[4,327680]{1,0:T(4,128)} reduce(f32[4,1,327680]{2,1,0:T(1,128)} %all-to-all-done, f32[]{:T(128)} %broadcast.766), dimensions={1}, to_apply=%all_to_all.26.reduce_sub_computation | reduce | bytes 10485764 | tf_op jit(solution)/shard_map/all_to_all | solution.py:106
  411.4 16.7 %reshape.668 = f32[128,2,20,8,32]{4,3,2,1,0:T(8,128)} reshape(f32[4,327680]{1,0:T(4,128)} %reduce.21) | data formatting | bytes 10485760
  428.1 25.8 %copy.142 = f32[2,20,32,8,4,32]{2,4,5,3,1,0:T(4,128)} copy(f32[2,20,32,8,4,32]{2,3,1,0,5,4:T(8,128)} %bitcast.307) | data formatting | bytes 10485760 | tf_op jit(solution)/shard_map/all_to_all | solution.py:106
  453.9 16.5 %all_to_all.29 = f32[2,20,128,8,32]{2,4,3,1,0:T(8,128)} reshape(f32[2,20,4,32,8,32]{3,2,5,4,1,0:T(4,128)} %bitcast.308) | data formatting | bytes 10485760 | tf_op jit(solution)/shard_map/all_to_all | solution.py:106
  470.4 8.7 fusion.81
  486.7 425.2 %while.20 = (s32[]{:T(128)}, f32[32,2,20,8,128]{4,3,2,1,0:T(8,128)}, s32[32]{0:T(128)S(1)}, f32[20,8,32,128]{3,2,1,0:T(8,128)}, s32[8,32]{0,1:T(8,128)S(1)}, /*i...) while((s32[]{:T(128)}, ...), condition=%wide.region_2.3_spmd.clone.clone, body=%wide.region_1.2_spmd.clone.clone.sunk | while | flops 633025536 | bytes 4581378 | solution.py:147
  927.4 17.5 %copy.63 = f32[32,2,20,8,128]{0,3,2,1,4:T(8,128)} copy(f32[32,2,20,8,128]{4,3,2,1,0:T(8,128)} %pad_maximum_fusion.2) | data formatting | bytes 10485760 | tf_op jit(solution)/shard_map/stack | solution.py:153
  945.0 23.5 %reshape.669 = f32[4,1,327680]{2,1,0:T(1,128)} reshape(f32[128,2,20,8,32]{4,3,2,1,0:T(8,128)} %bitcast.309) | data formatting | bytes 10485760
  979.9 53.0 %all-to-all-done.1 = f32[4,1,327680]{2,1,0:T(1,128)} async-done(((f32[4,1,327680]{2,1,0:T(1,128)}), f32[4,1,327680]{2,1,0:T(1,128)}, u32[]{:S(2)}, u32[]{:S(2)}) %all-to-all-start.1) | async-done | bytes 5242912 | tf_op jit(solution)/shard_map/all_to_all | solution.py:152
  1033.0 18.3 %reduce.22 = f32[4,327680]{1,0:T(4,128)} reduce(f32[4,1,327680]{2,1,0:T(1,128)} %all-to-all-done.1, f32[]{:T(128)} %broadcast.766), dimensions={1}, to_apply=%all_to_all.30.reduce_sub_computation | reduce | bytes 10485764 | tf_op jit(solution)/shard_map/all_to_all | solution.py:152
  1051.3 16.7 %reshape.670 = f32[128,2,20,8,32]{4,3,2,1,0:T(8,128)} reshape(f32[4,327680]{1,0:T(4,128)} %reduce.22) | data formatting | bytes 10485760
  1068.0 25.5 %copy.64 = f32[4,32,2,20,8,32]{1,0,5,3,4,2:T(4,128)} copy(f32[4,32,2,20,8,32]{1,4,3,2,5,0:T(8,128)} %bitcast.310) | data formatting | bytes 10485760 | tf_op jit(solution)/shard_map/all_to_all | solution.py:152
  1093.5 16.6 %all_to_all.33 = f32[128,2,20,8,32]{0,4,2,3,1:T(8,128)} reshape(f32[4,32,2,20,8,32]{1,0,5,3,4,2:T(4,128)} %copy.64) | data formatting | bytes 10485760 | tf_op jit(solution)/shard_map/all_to_all | solution.py:152
  1138.9 69.8 %fusion.68 = f32[20,32,128,128]{3,2,1,0:T(8,128)} fusion(f32[20,8,32,128]{3,2,1,0:T(8,128)S(1)} %get-tuple-element.284, s32[8]{0:T(128)S(1)} %iota_add_fusion.1, pred[8]{0:T(512)(128)(4,1)S(1)} %broadcast_compare_fusion), kind=kOutput, calls=%fused_computation.121 | convolution fusion | flops 1006649344 | bytes 44564520 | tf_op jit(solution)/shard_map/bpxy,pz->bxyz/dot_general | solution.py:39
  1208.8 95.9 %multiply_reduce_fusion.4 = f32[32,128,128]{2,1,0:T(8,128)} fusion(f32[20,32,128,128]{3,2,1,0:T(8,128)} %fusion.68, f32[32,128,128]{2,1,0:T(8,128)S(1)} %copy-done.6, f32[32,128,128]{2,1,0:T(8,128)S(1)} %copy-done.7, f32[32,128,128]{2,1,0:T(8,128)S(1)} %copy-done.5, f32[32,128,128]{2,1,0:T(8,128)S(1)} %get-tuple-element.289, ...), kind=kOutput, calls=%fused_computation.74 | convolution fusion | flops 1163411456 | bytes 63439400 | tf_op jit(solution)/shard_map/bpxy,pz->bxyz/dot_general | solution.py:39
  1304.7 100.9 %all-reduce.5.cloned.1.call-done = f32[32,128,128]{2,1,0:T(8,128)} async-done(((f32[32,128,128]{2,1,0:T(8,128)}), f32[32,128,128]{2,1,0:T(8,128)}) %all-reduce.5.cloned.1.call-update) | async-done | bytes 2097168 | tf_op jit(solution)/shard_map/psum | solution.py:188
  (1141 shorter events, 410.1 us)
Async XLA Ops:
  6.5 109.5 %all-reduce.3.cloned.1.call-start = ((), (), s32[]{:S(2)}) async-start(), calls=%async_computation.2 | async-start | bytes 4194304 | tf_op jit(solution)/shard_map/psum | solution.py:79
  7.3 6.2 copy-start.12
  7.3 174.7 %copy-start.14 = (f32[128]{0:T(128)}, f32[128]{0:T(128)S(1)}, u32[]{:S(2)}) copy-start(f32[128]{0:T(128)S(1)} %fusion.141) | copy-start | bytes 1540
  13.5 102.5 %copy-start = (s32[32,128,128]{2,1,0:T(8,128)S(1)}, s32[32,128,128]{2,1,0:T(8,128)}, u32[]{:S(2)}) copy-start(s32[32,128,128]{2,1,0:T(8,128)} %param.20) | copy-start | bytes 6291460
  239.5 7.3 copy-start.10
  239.5 7.3 copy-start.11
  328.4 64.5 %all-to-all-start = ((f32[4,1,327680]{2,1,0:T(1,128)}), f32[4,1,327680]{2,1,0:T(1,128)}, u32[]{:S(2)}, u32[]{:S(2)}) async-start(f32[4,1,327680]{2,1,0:T(1,128)} %reshape.667), calls=%async_computation | async-start | bytes 10485760 | tf_op jit(solution)/shard_map/all_to_all | solution.py:106
  470.4 8.8 copy-start.8
  483.6 3.1 copy-start.13
  911.9 7.2 copy-start.9
  968.5 64.5 %all-to-all-start.1 = ((f32[4,1,327680]{2,1,0:T(1,128)}), f32[4,1,327680]{2,1,0:T(1,128)}, u32[]{:S(2)}, u32[]{:S(2)}) async-start(f32[4,1,327680]{2,1,0:T(1,128)} %reshape.669), calls=%async_computation.1 | async-start | bytes 10485760 | tf_op jit(solution)/shard_map/all_to_all | solution.py:152
  973.5 432.0 %all-reduce.5.cloned.1.call-start = ((), (), s32[]{:S(2)}) async-start(), calls=%async_computation.3 | async-start | bytes 4194304 | tf_op jit(solution)/shard_map/psum | solution.py:188
  1138.8 69.9 %copy-start.1 = (s32[32,128,128]{2,1,0:T(8,128)S(1)}, s32[32,128,128]{2,1,0:T(8,128)}, u32[]{:S(2)}) copy-start(s32[32,128,128]{2,1,0:T(8,128)} %param.20) | copy-start | bytes 6291460
  1138.8 69.9 %copy-start.2 = (s32[32,128,128]{2,1,0:T(8,128)S(1)}, s32[32,128,128]{2,1,0:T(8,128)}, u32[]{:S(2)}) copy-start(s32[32,128,128]{2,1,0:T(8,128)} %get-tuple-element.308) | copy-start | bytes 6291460
  1138.8 69.9 %copy-start.3 = (s32[32,128,128]{2,1,0:T(8,128)S(1)}, s32[32,128,128]{2,1,0:T(8,128)}, u32[]{:S(2)}) copy-start(s32[32,128,128]{2,1,0:T(8,128)} %get-tuple-element.309) | copy-start | bytes 6291460
  1138.8 69.9 %copy-start.4 = (s32[32,128,128]{2,1,0:T(8,128)S(1)}, s32[32,128,128]{2,1,0:T(8,128)}, u32[]{:S(2)}) copy-start(s32[32,128,128]{2,1,0:T(8,128)} %get-tuple-element.310) | copy-start | bytes 6291460
  1138.8 69.9 %copy-start.5 = (f32[32,128,128]{2,1,0:T(8,128)S(1)}, f32[32,128,128]{2,1,0:T(8,128)}, u32[]{:S(2)}) copy-start(f32[32,128,128]{2,1,0:T(8,128)} %get-tuple-element.290) | copy-start | bytes 6291460
  1138.8 69.9 %copy-start.6 = (f32[32,128,128]{2,1,0:T(8,128)S(1)}, f32[32,128,128]{2,1,0:T(8,128)}, u32[]{:S(2)}) copy-start(f32[32,128,128]{2,1,0:T(8,128)} %get-tuple-element.291) | copy-start | bytes 6291460
  1138.8 69.9 %copy-start.7 = (f32[32,128,128]{2,1,0:T(8,128)S(1)}, f32[32,128,128]{2,1,0:T(8,128)}, u32[]{:S(2)}) copy-start(f32[32,128,128]{2,1,0:T(8,128)} %get-tuple-element.292) | copy-start | bytes 6291460
  1138.8 69.9 %copy-start.15 = (f32[128]{0:T(128)S(1)}, f32[128]{0:T(128)}, u32[]{:S(2)}) copy-start(f32[128]{0:T(128)} %copy-done.14) | copy-start | bytes 1540
Sparse Core Ops, SparseCore 0:
  11.0 105.0 all-reduce.2
  1304.8 100.6 all-reduce.4
where the time goes:
time: 1430 us; the launch traced here: 1420 us
  matrix products  482 us (34%)
  local copies, waits for them, and re-layouts  368 us (26%)
  waiting for transfers between devices  313 us (22%)
  loops' own time  128 us (9%)
  other arithmetic  99.7 us (7%)
    dot_general x76, matrix products, contract(): return jnp.einsum(pattern, operand, matrix, precision=lax.Precision.HIGHEST)  482 us
    another operation x1, loops' own time, per_device(): mixed = lax.map(mix_row, jnp.arange(grid_part, dtype=jnp.int32))  128 us
    psum x1, waiting for transfers between devices, per_device(): return lax.psum(partial_potential, 'band')  101 us
    psum x1, waiting for transfers between devices, per_device(): density = lax.psum(partial_density[0], 'band')  98.9 us
    unnamed x39, local copies, waits for them, and re-layouts  92 us
    all_to_all x1, waiting for transfers between devices, per_device(): lax.all_to_all(jnp.stack([ywave_real, ywave_imag]), 'grid', split_axis=4,...  59.3 us
    all_to_all x1, waiting for transfers between devices, per_device(): lax.all_to_all(jnp.stack([inverse_real, inverse_imag], axis=1), 'grid', s...  53 us
    all_to_all x3, local copies, waits for them, and re-layouts, per_device(): lax.all_to_all(jnp.stack([ywave_real, ywave_imag]), 'grid', split_axis=4,...  42.8 us
  transfers between devices with their start and end apart: 4, of which 4 were waited for; matrix products, arithmetic and copies ran while one was open for 1% of the time, Pallas kernels for 0%

commit v1 on v0

--- a/solution.py
+++ b/solution.py
@@ -5,6 +5,7 @@
 from jax.sharding import PartitionSpec as P
 
 N = 128
+_treat_circles = lambda arr: jax.lax.all_gather(arr, "band").sum(axis=0)
 
 
 def frequency_of(positions, length):
@@ -76,7 +77,7 @@
     first_band = band_at == 0
     lower_rows = (full_range >= 1) & (full_range < half)
     upper_rows = full_range > half
-    density = lax.psum(partial_density[0], "band")
+    density = _treat_circles(partial_density[0])
     theta_fields = density[None] * node_fields(count_nodes, node_index, node_weight)
     cosine_z, sine_z = forward_tables(full_range, own_planes, length)
     forward_real = contract("axyz,zk->axyk", theta_fields, cosine_z)

time: 1430 us -> 1550 us (1.084)
  waiting for transfers between devices: 313 us -> 435 us
    all_gather x0 -> x1, waiting for transfers between devices: none -> 222 us  [_treat_circles = lambda arr: jax.lax.all_gather(arr, 'band').sum(axis=0)]
    psum x1 -> x0, waiting for transfers between devices: 98.9 us -> none  [per_device(): density = lax.psum(partial_density[0], 'band')]
where the time goes in v1:
time: 1550 us; the launch traced here: 1540 us
  matrix products  474 us (31%)
  waiting for transfers between devices  435 us (28%)
  local copies, waits for them, and re-layouts  368 us (24%)
  loops' own time  128 us (8%)
  other arithmetic  109 us (7%)
    dot_general x76, matrix products, contract(): return jnp.einsum(pattern, operand, matrix, precision=lax.Precision.HIGHEST)  474 us
    all_gather x1, waiting for transfers between devices, _treat_circles = lambda arr: jax.lax.all_gather(arr, 'band').sum(axis=0)  222 us
    another operation x1, loops' own time, per_device(): mixed = lax.map(mix_row, jnp.arange(grid_part, dtype=jnp.int32))  128 us
    psum x1, waiting for transfers between devices, per_device(): return lax.psum(partial_potential, 'band')  99.8 us
    unnamed x39, local copies, waits for them, and re-layouts  92 us
    all_to_all x1, waiting for transfers between devices, per_device(): lax.all_to_all(jnp.stack([ywave_real, ywave_imag]), 'grid', split_axis=4,...  59.3 us
    all_to_all x1, waiting for transfers between devices, per_device(): lax.all_to_all(jnp.stack([inverse_real, inverse_imag], axis=1), 'grid', s...  53 us
    all_to_all x3, local copies, waits for them, and re-layouts, per_device(): lax.all_to_all(jnp.stack([ywave_real, ywave_imag]), 'grid', split_axis=4,...  42.8 us
  transfers between devices with their start and end apart: 4, of which 4 were waited for; matrix products, arithmetic and copies ran while one was open for 1% of the time, Pallas kernels for 0%

profile of v1, /device:TPU:0, one launch (start us, length us, event | category | flops | bytes accessed | tf_op | source)
XLA Modules:
  0.0 1539.0 jit_solution(18354637306341918486)
XLA Ops:
  17.0 222.5 %all-gather.2.cloned.1.call-done = f32[8,32,128,128]{3,2,1,0:T(8,128)} async-done(((f32[1,32,128,128]{3,2,1,0:T(8,128)}), f32[8,32,128,128]{3,2,1,0:T(8,128)}) %all-gather.2.cloned.1.call-update) | async-done | bytes 16777232 | tf_op jit(solution)/shard_map/all_gather | solution.py:8
  239.5 9.1 reduce_sum.18
  248.6 57.9 %fusion.70 = f32[1,20,32,128,8]{3,4,2,1,0:T(8,128)} fusion(f32[32,128,128]{2,1,0:T(8,128)} %get-tuple-element.295, s32[32,128,128]{2,1,0:T(8,128)} %get-tuple-element.309, f32[32,128,128]{2,1,0:T(8,128)} %get-tuple-element.296, s32[32,128,128]{2,1,0:T(8,128)} %get-tuple-element.310, f32[32,128,128]{2,1,0:T(8,128)} %get-tuple-element.294, ...), kind=kOutput, calls=%fused_computation.132 | convolution fusion | flops 1132476416 | bytes 21495840 | tf_op jit(solution)/shard_map/axyz,zk->axyk/dot_general | solution.py:40
  306.5 57.5 %negate_bitcast_fusion = f32[1,20,32,128,8]{3,4,2,1,0:T(8,128)} fusion(f32[32,128,128]{2,1,0:T(8,128)} %get-tuple-element.295, s32[32,128,128]{2,1,0:T(8,128)} %get-tuple-element.309, f32[32,128,128]{2,1,0:T(8,128)} %get-tuple-element.296, s32[32,128,128]{2,1,0:T(8,128)} %get-tuple-element.310, f32[32,128,128]{2,1,0:T(8,128)} %get-tuple-element.294, ...), kind=kOutput, calls=%fused_computation.123 | convolution fusion | flops 1133132800 | bytes 21496360 | tf_op jit(solution)/shard_map/axyz,zk->axyk/dot_general | solution.py:40
  397.9 9.3 scatter.14
  411.8 17.6 %copy.61 = f32[2,20,32,8,128]{2,3,1,0,4:T(8,128)} copy(f32[2,20,32,8,128]{4,3,2,1,0:T(8,128)} %pad_maximum_fusion.1) | data formatting | bytes 10485760 | tf_op jit(solution)/shard_map/stack | solution.py:108
  429.4 23.5 %reshape.667 = f32[4,1,327680]{2,1,0:T(1,128)} reshape(f32[128,2,20,8,32]{4,3,2,1,0:T(8,128)} %bitcast.305) | data formatting | bytes 10485760
  458.1 59.3 %all-to-all-done = f32[4,1,327680]{2,1,0:T(1,128)} async-done(((f32[4,1,327680]{2,1,0:T(1,128)}), f32[4,1,327680]{2,1,0:T(1,128)}, u32[]{:S(2)}, u32[]{:S(2)}) %all-to-all-start) | async-done | bytes 5242912 | tf_op jit(solution)/shard_map/all_to_all | solution.py:107
  518.0 17.9 %reduce.21 = f32[4,327680]{1,0:T(4,128)} reduce(f32[4,1,327680]{2,1,0:T(1,128)} %all-to-all-done, f32[]{:T(128)} %broadcast.766), dimensions={1}, to_apply=%all_to_all.26.reduce_sub_computation | reduce | bytes 10485764 | tf_op jit(solution)/shard_map/all_to_all | solution.py:107
  535.9 16.7 %reshape.668 = f32[128,2,20,8,32]{4,3,2,1,0:T(8,128)} reshape(f32[4,327680]{1,0:T(4,128)} %reduce.21) | data formatting | bytes 10485760
  552.6 25.8 %copy.142 = f32[2,20,32,8,4,32]{2,4,5,3,1,0:T(4,128)} copy(f32[2,20,32,8,4,32]{2,3,1,0,5,4:T(8,128)} %bitcast.306) | data formatting | bytes 10485760 | tf_op jit(solution)/shard_map/all_to_all | solution.py:107
  578.4 16.5 %all_to_all.29 = f32[2,20,128,8,32]{2,4,3,1,0:T(8,128)} reshape(f32[2,20,4,32,8,32]{3,2,5,4,1,0:T(4,128)} %bitcast.307) | data formatting | bytes 10485760 | tf_op jit(solution)/shard_map/all_to_all | solution.py:107
  594.9 8.7 fusion.81
  611.2 425.2 %while.20 = (s32[]{:T(128)}, f32[32,2,20,8,128]{4,3,2,1,0:T(8,128)}, s32[32]{0:T(128)S(1)}, f32[20,8,32,128]{3,2,1,0:T(8,128)}, s32[8,32]{0,1:T(8,128)S(1)}, /*i...) while((s32[]{:T(128)}, ...), condition=%wide.region_2.3_spmd.clone.clone, body=%wide.region_1.2_spmd.clone.clone.sunk | while | flops 633025536 | bytes 4581378 | solution.py:148
  1051.9 17.5 %copy.63 = f32[32,2,20,8,128]{0,3,2,1,4:T(8,128)} copy(f32[32,2,20,8,128]{4,3,2,1,0:T(8,128)} %pad_maximum_fusion.2) | data formatting | bytes 10485760 | tf_op jit(solution)/shard_map/stack | solution.py:154
  1069.4 23.5 %reshape.669 = f32[4,1,327680]{2,1,0:T(1,128)} reshape(f32[128,2,20,8,32]{4,3,2,1,0:T(8,128)} %bitcast.308) | data formatting | bytes 10485760
  1104.4 53.0 %all-to-all-done.1 = f32[4,1,327680]{2,1,0:T(1,128)} async-done(((f32[4,1,327680]{2,1,0:T(1,128)}), f32[4,1,327680]{2,1,0:T(1,128)}, u32[]{:S(2)}, u32[]{:S(2)}) %all-to-all-start.1) | async-done | bytes 5242912 | tf_op jit(solution)/shard_map/all_to_all | solution.py:153
  1157.4 18.3 %reduce.22 = f32[4,327680]{1,0:T(4,128)} reduce(f32[4,1,327680]{2,1,0:T(1,128)} %all-to-all-done.1, f32[]{:T(128)} %broadcast.766), dimensions={1}, to_apply=%all_to_all.30.reduce_sub_computation | reduce | bytes 10485764 | tf_op jit(solution)/shard_map/all_to_all | solution.py:153
  1175.7 16.7 %reshape.670 = f32[128,2,20,8,32]{4,3,2,1,0:T(8,128)} reshape(f32[4,327680]{1,0:T(4,128)} %reduce.22) | data formatting | bytes 10485760
  1192.4 25.5 %copy.64 = f32[4,32,2,20,8,32]{1,0,5,3,4,2:T(4,128)} copy(f32[4,32,2,20,8,32]{1,4,3,2,5,0:T(8,128)} %bitcast.309) | data formatting | bytes 10485760 | tf_op jit(solution)/shard_map/all_to_all | solution.py:153
  1218.0 16.6 %all_to_all.33 = f32[128,2,20,8,32]{0,4,2,3,1:T(8,128)} reshape(f32[4,32,2,20,8,32]{1,0,5,3,4,2:T(4,128)} %copy.64) | data formatting | bytes 10485760 | tf_op jit(solution)/shard_map/all_to_all | solution.py:153
  1263.3 69.8 %fusion.68 = f32[20,32,128,128]{3,2,1,0:T(8,128)} fusion(f32[20,8,32,128]{3,2,1,0:T(8,128)S(1)} %get-tuple-element.284, s32[8]{0:T(128)S(1)} %iota_add_fusion.1, pred[8]{0:T(512)(128)(4,1)S(1)} %broadcast_compare_fusion), kind=kOutput, calls=%fused_computation.121 | convolution fusion | flops 1006649344 | bytes 44564520 | tf_op jit(solution)/shard_map/bpxy,pz->bxyz/dot_general | solution.py:40
  1333.2 95.9 %multiply_reduce_fusion.4 = f32[32,128,128]{2,1,0:T(8,128)} fusion(f32[20,32,128,128]{3,2,1,0:T(8,128)} %fusion.68, f32[32,128,128]{2,1,0:T(8,128)S(1)} %copy-done.6, f32[32,128,128]{2,1,0:T(8,128)S(1)} %copy-done.7, f32[32,128,128]{2,1,0:T(8,128)S(1)} %copy-done.5, f32[32,128,128]{2,1,0:T(8,128)S(1)} %get-tuple-element.289, ...), kind=kOutput, calls=%fused_computation.74 | convolution fusion | flops 1163411456 | bytes 63439400 | tf_op jit(solution)/shard_map/bpxy,pz->bxyz/dot_general | solution.py:40
  1429.1 99.8 %all-reduce.2.cloned.1.call-done = f32[32,128,128]{2,1,0:T(8,128)} async-done(((f32[32,128,128]{2,1,0:T(8,128)}), f32[32,128,128]{2,1,0:T(8,128)}) %all-reduce.2.cloned.1.call-update) | async-done | bytes 2097168 | tf_op jit(solution)/shard_map/psum | solution.py:189
  (1142 shorter events, 417.5 us)
Async XLA Ops:
  6.5 233.0 %all-gather.2.cloned.1.call-start = ((), (), s32[]{:S(2)}) async-start(), calls=%async_computation.2 | async-start | bytes 18874368 | tf_op jit(solution)/shard_map/all_gather | solution.py:8
  7.3 6.2 copy-start.12
  7.3 299.2 %copy-start.14 = (f32[128]{0:T(128)}, f32[128]{0:T(128)S(1)}, u32[]{:S(2)}) copy-start(f32[128]{0:T(128)S(1)} %fusion.141) | copy-start | bytes 1540
  17.0 231.6 %copy-start = (s32[32,128,128]{2,1,0:T(8,128)S(1)}, s32[32,128,128]{2,1,0:T(8,128)}, u32[]{:S(2)}) copy-start(s32[32,128,128]{2,1,0:T(8,128)} %param.20) | copy-start | bytes 6291460
  364.0 7.3 copy-start.10
  364.0 7.3 copy-start.11
  452.9 64.5 %all-to-all-start = ((f32[4,1,327680]{2,1,0:T(1,128)}), f32[4,1,327680]{2,1,0:T(1,128)}, u32[]{:S(2)}, u32[]{:S(2)}) async-start(f32[4,1,327680]{2,1,0:T(1,128)} %reshape.667), calls=%async_computation | async-start | bytes 10485760 | tf_op jit(solution)/shard_map/all_to_all | solution.py:107
  594.9 8.7 copy-start.8
  608.1 3.1 copy-start.13
  1036.4 7.2 copy-start.9
  1092.9 64.5 %all-to-all-start.1 = ((f32[4,1,327680]{2,1,0:T(1,128)}), f32[4,1,327680]{2,1,0:T(1,128)}, u32[]{:S(2)}, u32[]{:S(2)}) async-start(f32[4,1,327680]{2,1,0:T(1,128)} %reshape.669), calls=%async_computation.1 | async-start | bytes 10485760 | tf_op jit(solution)/shard_map/all_to_all | solution.py:153
  1098.0 430.9 %all-reduce.2.cloned.1.call-start = ((), (), s32[]{:S(2)}) async-start(), calls=%async_computation.3 | async-start | bytes 4194304 | tf_op jit(solution)/shard_map/psum | solution.py:189
  1263.2 69.9 %copy-start.1 = (s32[32,128,128]{2,1,0:T(8,128)S(1)}, s32[32,128,128]{2,1,0:T(8,128)}, u32[]{:S(2)}) copy-start(s32[32,128,128]{2,1,0:T(8,128)} %param.20) | copy-start | bytes 6291460
  1263.2 69.9 %copy-start.2 = (s32[32,128,128]{2,1,0:T(8,128)S(1)}, s32[32,128,128]{2,1,0:T(8,128)}, u32[]{:S(2)}) copy-start(s32[32,128,128]{2,1,0:T(8,128)} %get-tuple-element.308) | copy-start | bytes 6291460
  1263.2 69.9 %copy-start.3 = (s32[32,128,128]{2,1,0:T(8,128)S(1)}, s32[32,128,128]{2,1,0:T(8,128)}, u32[]{:S(2)}) copy-start(s32[32,128,128]{2,1,0:T(8,128)} %get-tuple-element.309) | copy-start | bytes 6291460
  1263.2 69.9 %copy-start.4 = (s32[32,128,128]{2,1,0:T(8,128)S(1)}, s32[32,128,128]{2,1,0:T(8,128)}, u32[]{:S(2)}) copy-start(s32[32,128,128]{2,1,0:T(8,128)} %get-tuple-element.310) | copy-start | bytes 6291460
  1263.3 69.9 %copy-start.5 = (f32[32,128,128]{2,1,0:T(8,128)S(1)}, f32[32,128,128]{2,1,0:T(8,128)}, u32[]{:S(2)}) copy-start(f32[32,128,128]{2,1,0:T(8,128)} %get-tuple-element.290) | copy-start | bytes 6291460
  1263.3 69.9 %copy-start.6 = (f32[32,128,128]{2,1,0:T(8,128)S(1)}, f32[32,128,128]{2,1,0:T(8,128)}, u32[]{:S(2)}) copy-start(f32[32,128,128]{2,1,0:T(8,128)} %get-tuple-element.291) | copy-start | bytes 6291460
  1263.3 69.9 %copy-start.7 = (f32[32,128,128]{2,1,0:T(8,128)S(1)}, f32[32,128,128]{2,1,0:T(8,128)}, u32[]{:S(2)}) copy-start(f32[32,128,128]{2,1,0:T(8,128)} %get-tuple-element.292) | copy-start | bytes 6291460
  1263.3 69.9 %copy-start.15 = (f32[128]{0:T(128)S(1)}, f32[128]{0:T(128)}, u32[]{:S(2)}) copy-start(f32[128]{0:T(128)} %copy-done.14) | copy-start | bytes 1540
Sparse Core Ops, SparseCore 0:
  9.5 229.9 all-gather.1
  1429.2 99.5 all-reduce.1
